TPU v7x, 32 devices: a whole 2x2x4 slice. The times are simulated.
32 devices in a mesh: dev: 32 (over z, y, x, core).
Axes of the slice: x: 2, y: 2, z: 4, core: 2. Of those that a mesh axis runs over, the one named last changes fastest.
Arguments:
- gauss_params: float32 [59, 262144], P(None, 'dev'), may hold values from -8 to 8, as said below
- adam_first: float32 [59, 262144], P(None, 'dev'), may hold values from -6 to 6
- adam_second: float32 [59, 262144], P(None, 'dev'), may hold values from 0.0001 to 100
- camera: float32 [2, 6], replicated, may hold values from -0.004 to 0.004
- send_first: int32 [32, 4096], P('dev'), may hold values from -1 to 8191, as said below
- send_second: int32 [32, 4096], P('dev'), may hold values from -1 to 8191, as said below
- lists_first: int32 [1024, 128], P('dev'), may hold values from -1 to 4095, as said below
- lists_second: int32 [1024, 128], P('dev'), may hold values from -1 to 4095, as said below
- tiles_first: int32 [1024], P('dev'), may hold values from 0 to 1023, as said below
- tiles_second: int32 [1024], P('dev'), may hold values from 0 to 1023, as said below
- targets: float32 [1024, 3, 256], P('dev'), may hold values from 0 to 1
Outputs:
- new_params: float32 [59, 262144], P(None, 'dev')
- new_first: float32 [59, 262144], P(None, 'dev')
- new_second: float32 [59, 262144], P(None, 'dev')
- rendered_next: float32 [1024, 3, 256], P('dev')
Inputs may be any that keep to these rules, and one draw needn't show every extreme that they name: `gauss_params`: rows 0 to 2 hold a position, 3 to 5 log scales, 6 to 9 a quaternion (w, x, y, z) with w at least 1, 10 an opacity logit, 11 + 16 c + k the spherical-harmonic coefficient k of colour c. Every Gaussian lies at depth 1.4 or more in front of both cameras. `send_first`: row s holds, for each destination d in turn, 128 slots: local column indices of Gaussians of device s, the used ones first, then -1. Entries other than -1 in a row are distinct. Some destination gets 128 used slots from every device. `send_second`: same form as send_first, but unused slots (-1) may stand anywhere in a destination's run. Some destination gets 128 used slots from every device. `lists_first`: row r, rendered by device r // 32, lists in compositing order (front first) received slots s * 128 + k of that device (slot k from device s), only used slots, then -1 to the end. Every used slot of a device appears exactly once among its rows. Some rows have no -1. `lists_second`: same form as lists_first, for the next view and its send array. `tiles_first`: A permutation of the image's tiles. `tiles_second`: A permutation of the image's tiles.
All inputs are finite; a program needn't handle non-finite values.
Results may differ from a plain program's by a relative error of at most 0.0003.
Values sent between devices are 32-bit elements; how exact they have to be, the bound alone decides.
No kernel may reach another device: no remote copies, remote signals or barrier semaphores. Data moves between devices by JAX's collectives and lax.ppermute only.
A program may use at most 128 MiB of HBM per device.

v0:
```python
import jax
import jax.numpy as jnp
import numpy as np
from jax import lax
from jax.sharding import PartitionSpec as P

LIST_LEN = 128
TILE_PIXELS = 256
TILES_X = 128
tile_edge = 16
focal_length = 1000.0
blur_floor = 0.3
adam_epsilon = 1e-08
bias_first = 1.0 - 0.9**20
bias_second = 1.0 - 0.999**20
sh_first = 0.28209479177387814
sh_second = 0.4886025119029199
sh_third = (
    1.0925484305920792,
    -1.0925484305920792,
    0.31539156525252005,
    -1.0925484305920792,
    0.5462742152960396,
)
sh_fourth = (
    -0.5900435899266435,
    2.890611442640554,
    -0.4570457994644658,
    0.3731763325901154,
    -0.4570457994644658,
    1.445305721320277,
    -0.5900435899266435,
)


def rate_values():
    values = np.full((59,), 0.000125)
    values[0:3] = 0.00016
    values[3:6] = 0.005
    values[6:10] = 0.001
    values[10] = 0.05
    values[11] = 0.0025
    values[27] = 0.0025
    values[43] = 0.0025
    return values


def camera_frame(camera_row):
    cosine_a, sine_a = (jnp.cos(camera_row[0]), jnp.sin(camera_row[0]))
    cosine_b, sine_b = (jnp.cos(camera_row[1]), jnp.sin(camera_row[1]))
    cosine_c, sine_c = (jnp.cos(camera_row[2]), jnp.sin(camera_row[2]))
    filler_zero = jnp.zeros_like(cosine_a)
    filler_one = jnp.ones_like(cosine_a)
    turn_x = jnp.stack(
        [
            jnp.stack([filler_one, filler_zero, filler_zero]),
            jnp.stack([filler_zero, cosine_a, -sine_a]),
            jnp.stack([filler_zero, sine_a, cosine_a]),
        ]
    )
    turn_y = jnp.stack(
        [
            jnp.stack([cosine_b, filler_zero, sine_b]),
            jnp.stack([filler_zero, filler_one, filler_zero]),
            jnp.stack([-sine_b, filler_zero, cosine_b]),
        ]
    )
    turn_z = jnp.stack(
        [
            jnp.stack([cosine_c, -sine_c, filler_zero]),
            jnp.stack([sine_c, cosine_c, filler_zero]),
            jnp.stack([filler_zero, filler_zero, filler_one]),
        ]
    )
    highest = lax.Precision.HIGHEST
    rotation = jnp.dot(turn_z, jnp.dot(turn_y, turn_x, precision=highest), precision=highest)
    return (rotation, camera_row[3:6])


def sh_terms(along_x, along_y, along_z):
    square_x, square_y, square_z = (along_x * along_x, along_y * along_y, along_z * along_z)
    return [
        -sh_second * along_y,
        sh_second * along_z,
        -sh_second * along_x,
        sh_third[0] * along_x * along_y,
        sh_third[1] * along_y * along_z,
        sh_third[2] * (2.0 * square_z - square_x - square_y),
        sh_third[3] * along_x * along_z,
        sh_third[4] * (square_x - square_y),
        sh_fourth[0] * along_y * (3.0 * square_x - square_y),
        sh_fourth[1] * along_x * along_y * along_z,
        sh_fourth[2] * along_y * (4.0 * square_z - square_x - square_y),
        sh_fourth[3] * along_z * (2.0 * square_z - 3.0 * square_x - 3.0 * square_y),
        sh_fourth[4] * along_x * (4.0 * square_z - square_x - square_y),
        sh_fourth[5] * along_z * (square_x - square_y),
        sh_fourth[6] * along_x * (square_x - 3.0 * square_y),
    ]


def project(params, camera_row, image_width, image_height):
    rotation, offset = camera_frame(camera_row)
    centres = params[0:3]
    viewed = [
        rotation[row_index, 0] * centres[0]
        + rotation[row_index, 1] * centres[1]
        + rotation[row_index, 2] * centres[2]
        + offset[row_index]
        for row_index in range(3)
    ]
    inverse_depth = 1.0 / viewed[2]
    screen_u = focal_length * viewed[0] * inverse_depth + 0.5 * image_width
    screen_v = focal_length * viewed[1] * inverse_depth + 0.5 * image_height
    scales = jnp.exp(params[3:6])
    versor = params[6:10] / jnp.sqrt(jnp.sum(params[6:10] * params[6:10], axis=0))
    part_w, part_x, part_y, part_z = (versor[0], versor[1], versor[2], versor[3])
    turn_rows = [
        [
            1.0 - 2.0 * (part_y * part_y + part_z * part_z),
            2.0 * (part_x * part_y - part_w * part_z),
            2.0 * (part_x * part_z + part_w * part_y),
        ],
        [
            2.0 * (part_x * part_y + part_w * part_z),
            1.0 - 2.0 * (part_x * part_x + part_z * part_z),
            2.0 * (part_y * part_z - part_w * part_x),
        ],
        [
            2.0 * (part_x * part_z - part_w * part_y),
            2.0 * (part_y * part_z + part_w * part_x),
            1.0 - 2.0 * (part_x * part_x + part_y * part_y),
        ],
    ]
    factor = [
        [turn_rows[row_index][col_index] * scales[col_index] for col_index in range(3)]
        for row_index in range(3)
    ]
    spread = [
        [
            factor[row_index][0] * factor[col_index][0]
            + factor[row_index][1] * factor[col_index][1]
            + factor[row_index][2] * factor[col_index][2]
            for col_index in range(3)
        ]
        for row_index in range(3)
    ]
    jacobian = [
        [
            focal_length * inverse_depth,
            0.0,
            -focal_length * viewed[0] * inverse_depth * inverse_depth,
        ],
        [
            0.0,
            focal_length * inverse_depth,
            -focal_length * viewed[1] * inverse_depth * inverse_depth,
        ],
    ]
    mapping = [
        [
            jacobian[row_index][0] * rotation[0, col_index]
            + jacobian[row_index][1] * rotation[1, col_index]
            + jacobian[row_index][2] * rotation[2, col_index]
            for col_index in range(3)
        ]
        for row_index in range(2)
    ]

    def mapped(first_index, second_index):
        running = 0.0
        for inner_a in range(3):
            for inner_b in range(3):
                running = (
                    running
                    + mapping[first_index][inner_a]
                    * spread[inner_a][inner_b]
                    * mapping[second_index][inner_b]
                )
        return running

    cover_a = mapped(0, 0) + blur_floor
    cover_b = mapped(0, 1)
    cover_c = mapped(1, 1) + blur_floor
    determinant = cover_a * cover_c - cover_b * cover_b
    opacity = jax.nn.sigmoid(params[10])
    centre_cam = [
        -(
            rotation[0, col_index] * offset[0]
            + rotation[1, col_index] * offset[1]
            + rotation[2, col_index] * offset[2]
        )
        for col_index in range(3)
    ]
    towards = [centres[col_index] - centre_cam[col_index] for col_index in range(3)]
    length = jnp.sqrt(towards[0] * towards[0] + towards[1] * towards[1] + towards[2] * towards[2])
    harmonics = sh_terms(towards[0] / length, towards[1] / length, towards[2] / length)
    colours = []
    for channel in range(3):
        running = 0.5 + sh_first * params[11 + 16 * channel]
        for term_index in range(1, 16):
            running = running + harmonics[term_index - 1] * params[11 + 16 * channel + term_index]
        colours.append(jnp.maximum(running, 0.0))
    return jnp.stack(
        [
            screen_u,
            screen_v,
            cover_c / determinant,
            -cover_b / determinant,
            cover_a / determinant,
            opacity,
        ]
        + colours
    )


def composite(gathered, live_mask, tile_numbers, triangle):
    pixel_ids = jnp.arange(TILE_PIXELS, dtype=jnp.int32)
    pixel_col = (tile_numbers % TILES_X)[:, None] * tile_edge + pixel_ids[None, :] % tile_edge
    pixel_row = (tile_numbers // TILES_X)[:, None] * tile_edge + pixel_ids[None, :] // tile_edge
    offset_x = gathered[0][:, None, :] - (pixel_col.astype(gathered.dtype) + 0.5)[:, :, None]
    offset_y = gathered[1][:, None, :] - (pixel_row.astype(gathered.dtype) + 0.5)[:, :, None]
    exponent = (
        -0.5
        * (
            gathered[2][:, None, :] * offset_x * offset_x
            + gathered[4][:, None, :] * offset_y * offset_y
        )
        - gathered[3][:, None, :] * offset_x * offset_y
    )
    coverage = gathered[5][:, None, :] * jnp.exp(exponent) * live_mask[:, None, :]
    log_clear = jnp.log1p(-coverage)
    before = jnp.einsum("bpj,ji->bpi", log_clear, triangle, precision=lax.Precision.HIGHEST)
    weight = coverage * jnp.exp(before)
    return jnp.einsum("bpi,cbi->bcp", weight, gathered[6:9], precision=lax.Precision.HIGHEST)


def group_of():
    return 8


def selector(width, ids, dtype):
    return (jnp.arange(width, dtype=jnp.int32)[:, None] == ids[None, :]).astype(dtype)


def block_inputs(buffer, tile_lists):
    live_mask = (tile_lists >= 0).astype(buffer.dtype)
    safe_ids = jnp.maximum(tile_lists, 0).reshape(-1)
    choose = selector(buffer.shape[1], safe_ids, buffer.dtype)
    gathered = jnp.dot(buffer, choose, precision=lax.Precision.HIGHEST).reshape(
        buffer.shape[0], tile_lists.shape[0], LIST_LEN
    )
    return (gathered, live_mask, choose)


def train_tiles(buffer, tile_lists, tile_numbers, targets, triangle):
    tile_group = group_of()
    block_count = tile_lists.shape[0] // tile_group

    def train_one_block(running, pieces):
        piece_lists, piece_tiles, piece_targets = pieces
        gathered, live_mask, choose = block_inputs(buffer, piece_lists)

        def block_loss(splat_block):
            rendered = composite(splat_block, live_mask, piece_tiles, triangle)
            return 0.5 * jnp.sum((rendered - piece_targets) ** 2)

        splat_grad = jax.grad(block_loss)(gathered) * live_mask[None, :, :]
        splat_grad = splat_grad.reshape(buffer.shape[0], tile_group * LIST_LEN)
        return (
            running
            + lax.dot_general(
                splat_grad, choose, (((1,), (1,)), ((), ())), precision=lax.Precision.HIGHEST
            ),
            None,
        )

    pieces = (
        tile_lists.reshape(block_count, tile_group, LIST_LEN),
        tile_numbers.reshape(block_count, tile_group),
        targets.reshape(block_count, tile_group, 3, TILE_PIXELS),
    )
    running, unused = lax.scan(train_one_block, jnp.zeros(buffer.shape, buffer.dtype), pieces)
    return running


def render_tiles(buffer, tile_lists, tile_numbers, triangle):
    tile_group = group_of()
    block_count = tile_lists.shape[0] // tile_group

    def render_one_block(pieces):
        piece_lists, piece_tiles = pieces
        gathered, live_mask, choose = block_inputs(buffer, piece_lists)
        return composite(gathered, live_mask, piece_tiles, triangle)

    rendered = lax.map(
        render_one_block,
        (
            tile_lists.reshape(block_count, tile_group, LIST_LEN),
            tile_numbers.reshape(block_count, tile_group),
        ),
    )
    return rendered.reshape(tile_lists.shape[0], 3, TILE_PIXELS)


def slot_group():
    return 512


def pick_slots(source, slots):
    width = slot_group()
    blocks = slots.shape[0] // width
    safe_ids = jnp.maximum(slots, 0).reshape(blocks, width)

    def pick_one_block(block_ids):
        return jnp.dot(
            source,
            selector(source.shape[1], block_ids, source.dtype),
            precision=lax.Precision.HIGHEST,
        )

    picked = lax.map(pick_one_block, safe_ids)
    return jnp.transpose(picked, (1, 0, 2)).reshape(source.shape[0], slots.shape[0])


def return_slots(values, slots, local_count):
    width = slot_group()
    blocks = slots.shape[0] // width
    live = (slots >= 0).astype(values.dtype)
    masked = jnp.transpose(
        (values * live[None, :]).reshape(values.shape[0], blocks, width), (1, 0, 2)
    )
    safe_ids = jnp.maximum(slots, 0).reshape(blocks, width)

    def return_one_block(running, pieces):
        block_values, block_ids = pieces
        choose = selector(local_count, block_ids, values.dtype)
        return (
            running
            + lax.dot_general(
                block_values, choose, (((1,), (1,)), ((), ())), precision=lax.Precision.HIGHEST
            ),
            None,
        )

    total, unused = lax.scan(
        return_one_block,
        jnp.zeros((values.shape[0], local_count), values.dtype),
        (masked, safe_ids),
    )
    return total


def shards(
    gauss_params,
    adam_first,
    adam_second,
    camera,
    send_first,
    send_second,
    lists_first,
    lists_second,
    tiles_first,
    tiles_second,
    targets,
):
    devices = lax.axis_size("dev")
    image_width = TILES_X * tile_edge * 1.0
    image_height = lists_first.shape[0] * devices // TILES_X * tile_edge * 1.0
    local_count = gauss_params.shape[1]
    triangle = (jnp.arange(LIST_LEN)[:, None] < jnp.arange(LIST_LEN)[None, :]).astype(
        gauss_params.dtype
    )
    slots_first = send_first[0]
    picked = pick_slots(gauss_params, slots_first)

    def view_first(chosen):
        return project(chosen, camera[0], image_width, image_height)

    arrived = lax.all_to_all(picked, "dev", split_axis=1, concat_axis=1, tiled=True)
    buffer, pullback = jax.vjp(view_first, arrived)
    splat_grads = train_tiles(buffer, lists_first, tiles_first, targets, triangle)
    slot_grads = lax.all_to_all(
        pullback(splat_grads)[0], "dev", split_axis=1, concat_axis=1, tiled=True
    )
    gradient = return_slots(slot_grads, slots_first, local_count)
    new_first = 0.9 * adam_first + 0.1 * gradient
    new_second = 0.999 * adam_second + 0.001 * gradient * gradient
    step_sizes = jnp.asarray(rate_values(), gauss_params.dtype)[:, None]
    new_params = gauss_params - step_sizes * (new_first / bias_first) / (
        jnp.sqrt(new_second / bias_second) + adam_epsilon
    )
    picked_next = pick_slots(new_params, send_second[0])
    buffer_next = project(
        lax.all_to_all(picked_next, "dev", split_axis=1, concat_axis=1, tiled=True),
        camera[1],
        image_width,
        image_height,
    )
    rendered_next = render_tiles(buffer_next, lists_second, tiles_second, triangle)
    return (new_params, new_first, new_second, rendered_next)


def solution(mesh):
    placed = (
        P(None, "dev"),
        P(None, "dev"),
        P(None, "dev"),
        P(),
        P("dev", None),
        P("dev", None),
        P("dev", None),
        P("dev", None),
        P("dev"),
        P("dev"),
        P("dev", None, None),
    )
    return jax.shard_map(
        shards,
        mesh=mesh,
        in_specs=placed,
        out_specs=(P(None, "dev"), P(None, "dev"), P(None, "dev"), P("dev", None, None)),
        check_vma=False,
    )
```

profile of v0, /device:TPU:0, one launch (start us, length us, event | category | flops | bytes accessed | tf_op | source)
XLA Modules:
  0.0 493.7 jit_solution(3253605575347814456)
XLA Ops:
  1.6 60.9 %while.60 = (s32[]{:T(128)}, f32[8,59,512]{2,1,0:T(8,128)S(1)}, s32[8,512]{1,0:T(8,128)S(1)}, f32[59,8192]{1,0:T(8,128)}, s32[]{:T(128)}) while((s32[]{:T(128)}, f32[8,59,512]{2,1,0:T(8,128)S(1)}, s32[8,512]{1,0:T(8,128)S(1)}, f32[59,8192]{1,0:T(8,128)}, s32[]{:T(128)}) %tuple.414), condition=%wide.region_1.2_spmd, body=%wide.region_0.1_spmd.sunk | while | flops 2973761536 | bytes 2070597 | solution.py:321
  1.6 7.6 %fusion.409 = f32[8,59,512]{2,1,0:T(8,128)S(1)} fusion(f32[8,59,512]{2,1,0:T(8,128)S(1)} %get-tuple-element.1000, s32[]{:T(128)} %get-tuple-element.999, f32[59,8192]{1,0:T(8,128)} %get-tuple-element.1007, s32[512]{0:T(512)S(1)} %bitcast.1571), kind=kOutput, calls=%fused_computation.6.clone.1 | convolution fusion | flops 2973761536 | bytes 2066436 | tf_op jit(solution)/shard_map/while/body/eval_jaxpr/dot_general | solution.py:315
  9.2 7.6 %fusion.409 = f32[8,59,512]{2,1,0:T(8,128)S(1)} fusion(f32[8,59,512]{2,1,0:T(8,128)S(1)} %get-tuple-element.1000, s32[]{:T(128)} %get-tuple-element.999, f32[59,8192]{1,0:T(8,128)} %get-tuple-element.1007, s32[512]{0:T(512)S(1)} %bitcast.1571), kind=kOutput, calls=%fused_computation.6.clone.1 | convolution fusion | flops 2973761536 | bytes 2066436 | tf_op jit(solution)/shard_map/while/body/eval_jaxpr/dot_general | solution.py:315
  16.9 7.6 %fusion.409 = f32[8,59,512]{2,1,0:T(8,128)S(1)} fusion(f32[8,59,512]{2,1,0:T(8,128)S(1)} %get-tuple-element.1000, s32[]{:T(128)} %get-tuple-element.999, f32[59,8192]{1,0:T(8,128)} %get-tuple-element.1007, s32[512]{0:T(512)S(1)} %bitcast.1571), kind=kOutput, calls=%fused_computation.6.clone.1 | convolution fusion | flops 2973761536 | bytes 2066436 | tf_op jit(solution)/shard_map/while/body/eval_jaxpr/dot_general | solution.py:315
  24.5 7.6 %fusion.409 = f32[8,59,512]{2,1,0:T(8,128)S(1)} fusion(f32[8,59,512]{2,1,0:T(8,128)S(1)} %get-tuple-element.1000, s32[]{:T(128)} %get-tuple-element.999, f32[59,8192]{1,0:T(8,128)} %get-tuple-element.1007, s32[512]{0:T(512)S(1)} %bitcast.1571), kind=kOutput, calls=%fused_computation.6.clone.1 | convolution fusion | flops 2973761536 | bytes 2066436 | tf_op jit(solution)/shard_map/while/body/eval_jaxpr/dot_general | solution.py:315
  32.1 7.6 %fusion.409 = f32[8,59,512]{2,1,0:T(8,128)S(1)} fusion(f32[8,59,512]{2,1,0:T(8,128)S(1)} %get-tuple-element.1000, s32[]{:T(128)} %get-tuple-element.999, f32[59,8192]{1,0:T(8,128)} %get-tuple-element.1007, s32[512]{0:T(512)S(1)} %bitcast.1571), kind=kOutput, calls=%fused_computation.6.clone.1 | convolution fusion | flops 2973761536 | bytes 2066436 | tf_op jit(solution)/shard_map/while/body/eval_jaxpr/dot_general | solution.py:315
  39.7 7.6 %fusion.409 = f32[8,59,512]{2,1,0:T(8,128)S(1)} fusion(f32[8,59,512]{2,1,0:T(8,128)S(1)} %get-tuple-element.1000, s32[]{:T(128)} %get-tuple-element.999, f32[59,8192]{1,0:T(8,128)} %get-tuple-element.1007, s32[512]{0:T(512)S(1)} %bitcast.1571), kind=kOutput, calls=%fused_computation.6.clone.1 | convolution fusion | flops 2973761536 | bytes 2066436 | tf_op jit(solution)/shard_map/while/body/eval_jaxpr/dot_general | solution.py:315
  47.3 7.6 %fusion.409 = f32[8,59,512]{2,1,0:T(8,128)S(1)} fusion(f32[8,59,512]{2,1,0:T(8,128)S(1)} %get-tuple-element.1000, s32[]{:T(128)} %get-tuple-element.999, f32[59,8192]{1,0:T(8,128)} %get-tuple-element.1007, s32[512]{0:T(512)S(1)} %bitcast.1571), kind=kOutput, calls=%fused_computation.6.clone.1 | convolution fusion | flops 2973761536 | bytes 2066436 | tf_op jit(solution)/shard_map/while/body/eval_jaxpr/dot_general | solution.py:315
  54.9 7.6 %fusion.409 = f32[8,59,512]{2,1,0:T(8,128)S(1)} fusion(f32[8,59,512]{2,1,0:T(8,128)S(1)} %get-tuple-element.1000, s32[]{:T(128)} %get-tuple-element.999, f32[59,8192]{1,0:T(8,128)} %get-tuple-element.1007, s32[512]{0:T(512)S(1)} %bitcast.1571), kind=kOutput, calls=%fused_computation.6.clone.1 | convolution fusion | flops 2973761536 | bytes 2066436 | tf_op jit(solution)/shard_map/while/body/eval_jaxpr/dot_general | solution.py:315
  64.8 7.3 %all-to-all-start = ((f32[59,32,128]{2,0,1:T(8,128)}), f32[59,32,128]{2,0,1:T(8,128)S(1)}, u32[]{:S(2)}, u32[]{:S(2)}) async-start(f32[59,32,128]{2,0,1:T(8,128)} %copy.60), calls=%async_computation | async-start | bytes 2097152 | tf_op jit(solution)/shard_map/all_to_all | solution.py:379
  98.4 7.6 %broadcast_multiply_fusion.3 = (f32[1,32,128]{2,1,0:T(8,128)S(1)}, f32[1,32,128]{2,1,0:T(8,128)S(1)}, f32[1,32,128]{2,1,0:T(8,128)S(1)}, f32[1,32,128]{2,1,0:T(8...) fusion(f32[]{:T(128)} %bitcast.25, ...), kind=kLoop, calls=%fused_computation.629 | loop fusion | flops 102400 | bytes 196668 | tf_op jit(solution)/shard_map/jvp()/mul | solution.py:156
  110.5 94.4 %while.64 = (s32[]{:T(128)}, f32[9,4096]{1,0:T(8,128)S(1)}, s32[4,8,128]{2,1,0:T(8,128)S(1)}, f32[9,4096]{1,0:T(8,128)S(1)}, s32[4,8]{1,0:T(4,128)S(1)}, /*index...) while((s32[]{:T(128)}, f32[9,4096]{1,0:T(8,128)S(1)}, ...), condition=%wide.region_10.11_spmd.clone.clone, body=%wide.region_3.10_spmd.clone.clone.sunk | while | flops 1775461632 | bytes 7651711 | solution.py:282
  110.9 5.2 %fusion.432 = f32[9,1024]{1,0:T(8,128)S(1)} fusion(f32[9,4096]{1,0:T(8,128)S(1)} %get-tuple-element.1030, s32[1024]{0:T(1024)S(1)} %maximum_bitcast_fusion.5), kind=kOutput, calls=%fused_computation.103.clone.1 | convolution fusion | flops 457179136 | bytes 188416 | tf_op jit(solution)/shard_map/while/body/eval_jaxpr/dot_general | solution.py:249
  126.8 7.4 %fusion.436 = f32[9,4096]{1,0:T(8,128)S(1)} fusion(f32[9,1024]{1,0:T(8,128)S(1)} %bitcast.1480, s32[1024]{0:T(1024)S(1)} %maximum_bitcast_fusion.5, f32[9,4096]{1,0:T(8,128)S(1)} %get-tuple-element.1019, pred[]{:T(512)S(6)} %compare.134), kind=kOutput, calls=%fused_computation.82.clone.1 | convolution fusion | flops 457252864 | bytes 335873 | tf_op jit(solution)/shard_map/while/body/eval_jaxpr/dot_general | solution.py:271
  134.3 5.2 %fusion.432 = f32[9,1024]{1,0:T(8,128)S(1)} fusion(f32[9,4096]{1,0:T(8,128)S(1)} %get-tuple-element.1030, s32[1024]{0:T(1024)S(1)} %maximum_bitcast_fusion.5), kind=kOutput, calls=%fused_computation.103.clone.1 | convolution fusion | flops 457179136 | bytes 188416 | tf_op jit(solution)/shard_map/while/body/eval_jaxpr/dot_general | solution.py:249
  150.2 7.4 %fusion.436 = f32[9,4096]{1,0:T(8,128)S(1)} fusion(f32[9,1024]{1,0:T(8,128)S(1)} %bitcast.1480, s32[1024]{0:T(1024)S(1)} %maximum_bitcast_fusion.5, f32[9,4096]{1,0:T(8,128)S(1)} %get-tuple-element.1019, pred[]{:T(512)S(6)} %compare.134), kind=kOutput, calls=%fused_computation.82.clone.1 | convolution fusion | flops 457252864 | bytes 335873 | tf_op jit(solution)/shard_map/while/body/eval_jaxpr/dot_general | solution.py:271
  157.8 5.2 %fusion.432 = f32[9,1024]{1,0:T(8,128)S(1)} fusion(f32[9,4096]{1,0:T(8,128)S(1)} %get-tuple-element.1030, s32[1024]{0:T(1024)S(1)} %maximum_bitcast_fusion.5), kind=kOutput, calls=%fused_computation.103.clone.1 | convolution fusion | flops 457179136 | bytes 188416 | tf_op jit(solution)/shard_map/while/body/eval_jaxpr/dot_general | solution.py:249
  173.6 7.4 %fusion.436 = f32[9,4096]{1,0:T(8,128)S(1)} fusion(f32[9,1024]{1,0:T(8,128)S(1)} %bitcast.1480, s32[1024]{0:T(1024)S(1)} %maximum_bitcast_fusion.5, f32[9,4096]{1,0:T(8,128)S(1)} %get-tuple-element.1019, pred[]{:T(512)S(6)} %compare.134), kind=kOutput, calls=%fused_computation.82.clone.1 | convolution fusion | flops 457252864 | bytes 335873 | tf_op jit(solution)/shard_map/while/body/eval_jaxpr/dot_general | solution.py:271
  181.2 5.2 %fusion.432 = f32[9,1024]{1,0:T(8,128)S(1)} fusion(f32[9,4096]{1,0:T(8,128)S(1)} %get-tuple-element.1030, s32[1024]{0:T(1024)S(1)} %maximum_bitcast_fusion.5), kind=kOutput, calls=%fused_computation.103.clone.1 | convolution fusion | flops 457179136 | bytes 188416 | tf_op jit(solution)/shard_map/while/body/eval_jaxpr/dot_general | solution.py:249
  197.1 7.4 %fusion.436 = f32[9,4096]{1,0:T(8,128)S(1)} fusion(f32[9,1024]{1,0:T(8,128)S(1)} %bitcast.1480, s32[1024]{0:T(1024)S(1)} %maximum_bitcast_fusion.5, f32[9,4096]{1,0:T(8,128)S(1)} %get-tuple-element.1019, pred[]{:T(512)S(6)} %compare.134), kind=kOutput, calls=%fused_computation.82.clone.1 | convolution fusion | flops 457252864 | bytes 335873 | tf_op jit(solution)/shard_map/while/body/eval_jaxpr/dot_general | solution.py:271
  206.7 6.4 %broadcast_multiply_fusion.28 = (f32[1,4096]{1,0:T(1,128)S(1)}, f32[1,4096]{1,0:T(1,128)S(1)}, f32[1,4096]{1,0:T(1,128)S(1)}, f32[1,4096]{1,0:T(1,128)S(1)}, f32...) fusion(f32[]{:T(128)} %bitcast.35, f32[1,4096]{1,0:T(1,128)S(1)} %bitcast.1556, ...), kind=kLoop, calls=%fused_computation.661 | loop fusion | flops 585728 | bytes 884772 | tf_op jit(solution)/shard_map/transpose(jvp())/mul | solution.py:107
  226.9 5.2 %all-to-all-start.1 = ((f32[59,32,128]{2,0,1:T(8,128)}), f32[59,32,128]{2,0,1:T(8,128)S(1)}, u32[]{:S(2)}, u32[]{:S(2)}) async-start(f32[59,32,128]{2,0,1:T(8,128)} %copy.66), calls=%async_computation.1 | async-start | bytes 2097152 | tf_op jit(solution)/shard_map/all_to_all | solution.py:382
  232.2 26.1 %all-to-all-done.1 = f32[59,32,128]{2,0,1:T(8,128)S(1)} async-done(((f32[59,32,128]{2,0,1:T(8,128)}), f32[59,32,128]{2,0,1:T(8,128)S(1)}, u32[]{:S(2)}, u32[]{:S(2)}) %all-to-all-start.1) | async-done | bytes 966688 | tf_op jit(solution)/shard_map/all_to_all | solution.py:382
  259.1 86.1 %while.63 = (s32[]{:T(128)}, f32[59,8192]{1,0:T(8,128)}, f32[8,59,512]{2,0,1:T(8,128)S(1)}, s32[8,512]{1,0:T(8,128)S(1)}, s32[]{:T(128)}, /*index=5*/s32[]{:T(128)}) while((s32[]{:T(128)}, f32[59,8192]{1,0:T(8,128)}, f32[8,59,512]{2,0,1:T(8,128)S(1)}, s32[8,512]{1,0:T(8,128)S(1)}, s32[]{:T(128)}, /*index=5*/s32[]{:T(128)}) %tuple.432), condition=%wide.region_13.14_spmd.clone, body=%wide.region_12.13_spmd.clone.sunk | while | flops 2974728192 | bytes 4235351 | solution.py:345
  259.3 9.6 %fusion.421 = f32[59,8192]{1,0:T(8,128)} fusion(s32[512]{0:T(512)S(1)} %bitcast.1570, f32[59,8192]{1,0:T(8,128)} %get-tuple-element.1043, pred[]{:T(512)S(6)} %compare.133, f32[1,59,512]{2,0,1:T(1,128)S(1)} %constant_dynamic-slice_fusion.13), kind=kOutput, calls=%fused_computation.72.clone.1 | convolution fusion | flops 2974728192 | bytes 3989505 | tf_op jit(solution)/shard_map/while/body/eval_jaxpr/dot_general | solution.py:339
  269.0 10.8 %fusion.421 = f32[59,8192]{1,0:T(8,128)} fusion(s32[512]{0:T(512)S(1)} %bitcast.1570, f32[59,8192]{1,0:T(8,128)} %get-tuple-element.1043, pred[]{:T(512)S(6)} %compare.133, f32[1,59,512]{2,0,1:T(1,128)S(1)} %constant_dynamic-slice_fusion.13), kind=kOutput, calls=%fused_computation.72.clone.1 | convolution fusion | flops 2974728192 | bytes 3989505 | tf_op jit(solution)/shard_map/while/body/eval_jaxpr/dot_general | solution.py:339
  279.9 10.8 %fusion.421 = f32[59,8192]{1,0:T(8,128)} fusion(s32[512]{0:T(512)S(1)} %bitcast.1570, f32[59,8192]{1,0:T(8,128)} %get-tuple-element.1043, pred[]{:T(512)S(6)} %compare.133, f32[1,59,512]{2,0,1:T(1,128)S(1)} %constant_dynamic-slice_fusion.13), kind=kOutput, calls=%fused_computation.72.clone.1 | convolution fusion | flops 2974728192 | bytes 3989505 | tf_op jit(solution)/shard_map/while/body/eval_jaxpr/dot_general | solution.py:339
  290.8 10.8 %fusion.421 = f32[59,8192]{1,0:T(8,128)} fusion(s32[512]{0:T(512)S(1)} %bitcast.1570, f32[59,8192]{1,0:T(8,128)} %get-tuple-element.1043, pred[]{:T(512)S(6)} %compare.133, f32[1,59,512]{2,0,1:T(1,128)S(1)} %constant_dynamic-slice_fusion.13), kind=kOutput, calls=%fused_computation.72.clone.1 | convolution fusion | flops 2974728192 | bytes 3989505 | tf_op jit(solution)/shard_map/while/body/eval_jaxpr/dot_general | solution.py:339
  301.7 10.8 %fusion.421 = f32[59,8192]{1,0:T(8,128)} fusion(s32[512]{0:T(512)S(1)} %bitcast.1570, f32[59,8192]{1,0:T(8,128)} %get-tuple-element.1043, pred[]{:T(512)S(6)} %compare.133, f32[1,59,512]{2,0,1:T(1,128)S(1)} %constant_dynamic-slice_fusion.13), kind=kOutput, calls=%fused_computation.72.clone.1 | convolution fusion | flops 2974728192 | bytes 3989505 | tf_op jit(solution)/shard_map/while/body/eval_jaxpr/dot_general | solution.py:339
  312.7 10.8 %fusion.421 = f32[59,8192]{1,0:T(8,128)} fusion(s32[512]{0:T(512)S(1)} %bitcast.1570, f32[59,8192]{1,0:T(8,128)} %get-tuple-element.1043, pred[]{:T(512)S(6)} %compare.133, f32[1,59,512]{2,0,1:T(1,128)S(1)} %constant_dynamic-slice_fusion.13), kind=kOutput, calls=%fused_computation.72.clone.1 | convolution fusion | flops 2974728192 | bytes 3989505 | tf_op jit(solution)/shard_map/while/body/eval_jaxpr/dot_general | solution.py:339
  323.6 10.8 %fusion.421 = f32[59,8192]{1,0:T(8,128)} fusion(s32[512]{0:T(512)S(1)} %bitcast.1570, f32[59,8192]{1,0:T(8,128)} %get-tuple-element.1043, pred[]{:T(512)S(6)} %compare.133, f32[1,59,512]{2,0,1:T(1,128)S(1)} %constant_dynamic-slice_fusion.13), kind=kOutput, calls=%fused_computation.72.clone.1 | convolution fusion | flops 2974728192 | bytes 3989505 | tf_op jit(solution)/shard_map/while/body/eval_jaxpr/dot_general | solution.py:339
  334.5 10.8 %fusion.421 = f32[59,8192]{1,0:T(8,128)} fusion(s32[512]{0:T(512)S(1)} %bitcast.1570, f32[59,8192]{1,0:T(8,128)} %get-tuple-element.1043, pred[]{:T(512)S(6)} %compare.133, f32[1,59,512]{2,0,1:T(1,128)S(1)} %constant_dynamic-slice_fusion.13), kind=kOutput, calls=%fused_computation.72.clone.1 | convolution fusion | flops 2974728192 | bytes 3989505 | tf_op jit(solution)/shard_map/while/body/eval_jaxpr/dot_general | solution.py:339
  345.3 6.3 %divide_subtract_fusion = (f32[59,8192]{1,0:T(8,128)}, f32[59,8192]{1,0:T(8,128)}, f32[59,8192]{1,0:T(8,128)}) fusion(f32[59,8192]{1,0:T(8,128)S(1)} %copy-done, f32[59]{0:T(128)S(1)} %copy-done.7, f32[59,8192]{1,0:T(8,128)} %get-tuple-element.318, f32[59,8192]{1,0:T(8,128)} %param.23, f32[59,8192]{1,0:T(8,128)} %param.24), kind=kLoop, calls=%fused_computation.164 | loop fusion | flops 5799936 | bytes 13533420 | tf_op jit(solution)/shard_map/sub | solution.py:389
  351.7 60.9 %while.61 = (s32[]{:T(128)}, f32[8,59,512]{2,1,0:T(8,128)S(1)}, s32[8,512]{1,0:T(8,128)S(1)}, f32[59,8192]{1,0:T(8,128)}, s32[]{:T(128)}) while((s32[]{:T(128)}, f32[8,59,512]{2,1,0:T(8,128)S(1)}, s32[8,512]{1,0:T(8,128)S(1)}, f32[59,8192]{1,0:T(8,128)}, s32[]{:T(128)}) %tuple.423), condition=%wide.region_15.16_spmd, body=%wide.region_14.15_spmd.sunk | while | flops 2973761536 | bytes 2070597 | solution.py:321
  351.8 7.6 %fusion.411 = f32[8,59,512]{2,1,0:T(8,128)S(1)} fusion(f32[8,59,512]{2,1,0:T(8,128)S(1)} %get-tuple-element.1060, s32[]{:T(128)} %get-tuple-element.1059, f32[59,8192]{1,0:T(8,128)} %get-tuple-element.1067, s32[512]{0:T(512)S(1)} %bitcast.1572), kind=kOutput, calls=%fused_computation.12.clone.1 | convolution fusion | flops 2973761536 | bytes 2066436 | tf_op jit(solution)/shard_map/while/body/eval_jaxpr/dot_general | solution.py:315
  359.4 7.6 %fusion.411 = f32[8,59,512]{2,1,0:T(8,128)S(1)} fusion(f32[8,59,512]{2,1,0:T(8,128)S(1)} %get-tuple-element.1060, s32[]{:T(128)} %get-tuple-element.1059, f32[59,8192]{1,0:T(8,128)} %get-tuple-element.1067, s32[512]{0:T(512)S(1)} %bitcast.1572), kind=kOutput, calls=%fused_computation.12.clone.1 | convolution fusion | flops 2973761536 | bytes 2066436 | tf_op jit(solution)/shard_map/while/body/eval_jaxpr/dot_general | solution.py:315
  367.0 7.6 %fusion.411 = f32[8,59,512]{2,1,0:T(8,128)S(1)} fusion(f32[8,59,512]{2,1,0:T(8,128)S(1)} %get-tuple-element.1060, s32[]{:T(128)} %get-tuple-element.1059, f32[59,8192]{1,0:T(8,128)} %get-tuple-element.1067, s32[512]{0:T(512)S(1)} %bitcast.1572), kind=kOutput, calls=%fused_computation.12.clone.1 | convolution fusion | flops 2973761536 | bytes 2066436 | tf_op jit(solution)/shard_map/while/body/eval_jaxpr/dot_general | solution.py:315
  374.6 7.6 %fusion.411 = f32[8,59,512]{2,1,0:T(8,128)S(1)} fusion(f32[8,59,512]{2,1,0:T(8,128)S(1)} %get-tuple-element.1060, s32[]{:T(128)} %get-tuple-element.1059, f32[59,8192]{1,0:T(8,128)} %get-tuple-element.1067, s32[512]{0:T(512)S(1)} %bitcast.1572), kind=kOutput, calls=%fused_computation.12.clone.1 | convolution fusion | flops 2973761536 | bytes 2066436 | tf_op jit(solution)/shard_map/while/body/eval_jaxpr/dot_general | solution.py:315
  382.2 7.6 %fusion.411 = f32[8,59,512]{2,1,0:T(8,128)S(1)} fusion(f32[8,59,512]{2,1,0:T(8,128)S(1)} %get-tuple-element.1060, s32[]{:T(128)} %get-tuple-element.1059, f32[59,8192]{1,0:T(8,128)} %get-tuple-element.1067, s32[512]{0:T(512)S(1)} %bitcast.1572), kind=kOutput, calls=%fused_computation.12.clone.1 | convolution fusion | flops 2973761536 | bytes 2066436 | tf_op jit(solution)/shard_map/while/body/eval_jaxpr/dot_general | solution.py:315
  389.8 7.6 %fusion.411 = f32[8,59,512]{2,1,0:T(8,128)S(1)} fusion(f32[8,59,512]{2,1,0:T(8,128)S(1)} %get-tuple-element.1060, s32[]{:T(128)} %get-tuple-element.1059, f32[59,8192]{1,0:T(8,128)} %get-tuple-element.1067, s32[512]{0:T(512)S(1)} %bitcast.1572), kind=kOutput, calls=%fused_computation.12.clone.1 | convolution fusion | flops 2973761536 | bytes 2066436 | tf_op jit(solution)/shard_map/while/body/eval_jaxpr/dot_general | solution.py:315
  397.5 7.6 %fusion.411 = f32[8,59,512]{2,1,0:T(8,128)S(1)} fusion(f32[8,59,512]{2,1,0:T(8,128)S(1)} %get-tuple-element.1060, s32[]{:T(128)} %get-tuple-element.1059, f32[59,8192]{1,0:T(8,128)} %get-tuple-element.1067, s32[512]{0:T(512)S(1)} %bitcast.1572), kind=kOutput, calls=%fused_computation.12.clone.1 | convolution fusion | flops 2973761536 | bytes 2066436 | tf_op jit(solution)/shard_map/while/body/eval_jaxpr/dot_general | solution.py:315
  405.1 7.6 %fusion.411 = f32[8,59,512]{2,1,0:T(8,128)S(1)} fusion(f32[8,59,512]{2,1,0:T(8,128)S(1)} %get-tuple-element.1060, s32[]{:T(128)} %get-tuple-element.1059, f32[59,8192]{1,0:T(8,128)} %get-tuple-element.1067, s32[512]{0:T(512)S(1)} %bitcast.1572), kind=kOutput, calls=%fused_computation.12.clone.1 | convolution fusion | flops 2973761536 | bytes 2066436 | tf_op jit(solution)/shard_map/while/body/eval_jaxpr/dot_general | solution.py:315
  445.0 7.6 %broadcast_multiply_fusion.1 = (f32[1,32,128]{2,1,0:T(8,128)S(1)}, f32[1,32,128]{2,1,0:T(8,128)S(1)}, f32[1,32,128]{2,1,0:T(8,128)S(1)}, f32[1,32,128]{2,1,0:T(8...) fusion(f32[]{:T(128)} %bitcast.132, ...), kind=kLoop, calls=%fused_computation.627 | loop fusion | flops 98304 | bytes 180284 | tf_op jit(solution)/shard_map/mul | solution.py:156
  457.4 36.0 %while.62 = (s32[]{:T(128)}, f32[4,8,3,256]{3,1,0,2:T(8,128)}, s32[4,8,128]{2,1,0:T(8,128)S(1)}, f32[9,4096]{1,0:T(8,128)S(1)}, s32[4,8]{1,0:T(4,128)S(1)}, /*index=5*/s32[]{:T(128)}) while((s32[]{:T(128)}, f32[4,8,3,256]{3,1,0,2:T(8,128)}, s32[4,8,128]{2,1,0:T(8,128)S(1)}, f32[9,4096]{1,0:T(8,128)S(1)}, s32[4,8]{1,0:T(4,128)S(1)}, ...), condition=%wide.region_18.19_spmd.clone, body=%wide.region_17.18_spmd.clone.sunk | while | flops 876660928 | bytes 2507605 | solution.py:295
  457.6 5.2 %fusion.416 = f32[9,1024]{1,0:T(8,128)S(1)} fusion(f32[9,4096]{1,0:T(8,128)S(1)} %get-tuple-element.1084, s32[1024]{0:T(1024)S(1)} %maximum_bitcast_fusion.4), kind=kOutput, calls=%fused_computation.25.clone.1 | convolution fusion | flops 457179136 | bytes 188416 | tf_op jit(solution)/shard_map/while/body/eval_jaxpr/dot_general | solution.py:249
  466.6 5.2 %fusion.416 = f32[9,1024]{1,0:T(8,128)S(1)} fusion(f32[9,4096]{1,0:T(8,128)S(1)} %get-tuple-element.1084, s32[1024]{0:T(1024)S(1)} %maximum_bitcast_fusion.4), kind=kOutput, calls=%fused_computation.25.clone.1 | convolution fusion | flops 457179136 | bytes 188416 | tf_op jit(solution)/shard_map/while/body/eval_jaxpr/dot_general | solution.py:249
  475.6 5.2 %fusion.416 = f32[9,1024]{1,0:T(8,128)S(1)} fusion(f32[9,4096]{1,0:T(8,128)S(1)} %get-tuple-element.1084, s32[1024]{0:T(1024)S(1)} %maximum_bitcast_fusion.4), kind=kOutput, calls=%fused_computation.25.clone.1 | convolution fusion | flops 457179136 | bytes 188416 | tf_op jit(solution)/shard_map/while/body/eval_jaxpr/dot_general | solution.py:249
  484.6 5.2 %fusion.416 = f32[9,1024]{1,0:T(8,128)S(1)} fusion(f32[9,4096]{1,0:T(8,128)S(1)} %get-tuple-element.1084, s32[1024]{0:T(1024)S(1)} %maximum_bitcast_fusion.4), kind=kOutput, calls=%fused_computation.25.clone.1 | convolution fusion | flops 457179136 | bytes 188416 | tf_op jit(solution)/shard_map/while/body/eval_jaxpr/dot_general | solution.py:249
  (271 shorter events, 100.0 us)
Async XLA Ops:
  63.1 8.9 %copy-start.5 = (f32[2,6]{1,0:T(2,128)S(1)}, f32[2,6]{1,0:T(2,128)}, u32[]{:S(2)}) copy-start(f32[2,6]{1,0:T(2,128)} %param.25) | copy-start | bytes 148
  63.2 14.1 %copy-start.10 = (f32[1,3]{1,0:T(1,128)S(1)}, f32[1,3]{1,0:T(1,128)}, u32[]{:S(2)}) copy-start(f32[1,3]{1,0:T(1,128)} %constant.324.clone.1) | copy-start | bytes 40
  63.2 14.1 %copy-start.11 = (f32[1,3]{1,0:T(1,128)S(1)}, f32[1,3]{1,0:T(1,128)}, u32[]{:S(2)}) copy-start(f32[1,3]{1,0:T(1,128)} %constant.325.clone.1) | copy-start | bytes 40
  63.2 14.2 %copy-start.6 = (f32[1,3]{1,0:T(1,128)S(1)}, f32[1,3]{1,0:T(1,128)}, u32[]{:S(2)}) copy-start(f32[1,3]{1,0:T(1,128)} %constant.323.clone.1) | copy-start | bytes 40
  63.2 34.1 %copy-start.3 = (f32[32,3,256]{2,0,1:T(8,128)S(1)}, f32[32,3,256]{2,0,1:T(8,128)}, u32[]{:S(2)}) copy-start(f32[32,3,256]{2,0,1:T(8,128)} %param.32) | copy-start | bytes 294916
  63.2 34.1 %copy-start.8 = (s32[32]{0:T(128)S(1)}, s32[32]{0:T(128)}, u32[]{:S(2)}) copy-start(s32[32]{0:T(128)} %param.30) | copy-start | bytes 388
  64.8 33.5 %all-to-all-start = ((f32[59,32,128]{2,0,1:T(8,128)}), f32[59,32,128]{2,0,1:T(8,128)S(1)}, u32[]{:S(2)}, u32[]{:S(2)}) async-start(f32[59,32,128]{2,0,1:T(8,128)} %copy.60), calls=%async_computation | async-start | bytes 2097152 | tf_op jit(solution)/shard_map/all_to_all | solution.py:379
  92.2 18.3 %copy-start.1 = (s32[32,128]{1,0:T(8,128)S(1)}, s32[32,128]{1,0:T(8,128)}, u32[]{:S(2)}) copy-start(s32[32,128]{1,0:T(8,128)} %param.28) | copy-start | bytes 49156
  225.4 6.7 %copy-start.4 = (s32[1,4096]{1,0:T(1,128)S(1)}, s32[1,4096]{1,0:T(1,128)}, u32[]{:S(2)}) copy-start(s32[1,4096]{1,0:T(1,128)} %param.26) | copy-start | bytes 49156
  226.9 31.4 %all-to-all-start.1 = ((f32[59,32,128]{2,0,1:T(8,128)}), f32[59,32,128]{2,0,1:T(8,128)S(1)}, u32[]{:S(2)}, u32[]{:S(2)}) async-start(f32[59,32,128]{2,0,1:T(8,128)} %copy.66), calls=%async_computation.1 | async-start | bytes 2097152 | tf_op jit(solution)/shard_map/all_to_all | solution.py:382
  259.1 86.2 %copy-start = (f32[59,8192]{1,0:T(8,128)S(1)}, f32[59,8192]{1,0:T(8,128)}, u32[]{:S(2)}) copy-start(f32[59,8192]{1,0:T(8,128)} %get-tuple-element.1090) | copy-start | bytes 5799940
  259.1 86.2 %copy-start.7 = (f32[59]{0:T(128)S(1)}, f32[59]{0:T(128)}, u32[]{:S(2)}) copy-start(f32[59]{0:T(128)} %constant.528) | copy-start | bytes 712
  413.3 29.9 %copy-start.9 = (s32[32]{0:T(128)S(1)}, s32[32]{0:T(128)}, u32[]{:S(2)}) copy-start(s32[32]{0:T(128)} %param.31) | copy-start | bytes 388
  414.8 30.0 %all-to-all-start.2 = ((f32[59,32,128]{2,0,1:T(8,128)}), f32[59,32,128]{2,0,1:T(8,128)S(1)}, u32[]{:S(2)}, u32[]{:S(2)}) async-start(f32[59,32,128]{2,0,1:T(8,128)} %copy.70), calls=%async_computation.2 | async-start | bytes 2097152 | tf_op jit(solution)/shard_map/all_to_all | solution.py:394
  418.7 38.7 %copy-start.2 = (s32[32,128]{1,0:T(8,128)S(1)}, s32[32,128]{1,0:T(8,128)}, u32[]{:S(2)}) copy-start(s32[32,128]{1,0:T(8,128)} %param.29) | copy-start | bytes 49156
where the time goes:
time: 503 us; the launch traced here: 494 us
  matrix products  332 us (66%)
  other arithmetic  53.5 us (11%)
  between operations  48.2 us (10%)
  waiting for transfers between devices  28.5 us (6%)
  starting transfers between devices  16.3 us (3%)
  local copies, waits for them, and re-layouts  13.9 us (3%)
    dot_general x16, matrix products, pick_one_block(): jnp.dot(source, selector(source.shape[1], block_ids, source.dtype), preci...  121 us
    dot_general x8, matrix products, return_one_block(): lax.dot_general(block_values, choose, (((1,), (1,)), ((), ())), precision...  85.1 us
    dot_general x8, matrix products, block_inputs(): jnp.dot(buffer, choose, precision=lax.Precision.HIGHEST)  41.3 us
    dot_general x4, matrix products, train_one_block(): lax.dot_general(splat_grad, choose, (((1,), (1,)), ((), ())), precision=l...  29.6 us
    dot_general x12, matrix products, composite(): jnp.einsum('bpj,ji->bpi', log_clear, triangle, precision=lax.Precision.HI...  29.2 us
    all_to_all x1, waiting for transfers between devices, shards(): lax.all_to_all(pullback(splat_grads)[0], 'dev', split_axis=1, concat_axis...  26.1 us
    dot_general x16, matrix products, composite(): jnp.einsum('bpi,cbi->bcp', weight, gathered[6:9], precision=lax.Precision...  24.5 us
    mul x2, other arithmetic, project(): -focal_length * viewed[1] * inverse_depth * inverse_depth  15.2 us
  transfers between devices with their start and end apart: 3, of which 3 were waited for; matrix products, arithmetic and copies ran while one was open for 1% of the time, Pallas kernels for 0%

commit v1 on v0

--- a/solution.py
+++ b/solution.py
@@ -379,8 +379,14 @@
     arrived = lax.all_to_all(picked, "dev", split_axis=1, concat_axis=1, tiled=True)
     buffer, pullback = jax.vjp(view_first, arrived)
     splat_grads = train_tiles(buffer, lists_first, tiles_first, targets, triangle)
-    slot_grads = lax.all_to_all(
-        pullback(splat_grads)[0], "dev", split_axis=1, concat_axis=1, tiled=True
+    slot_grads = jnp.concatenate(
+        lax.all_to_all(
+            jnp.stack(jnp.split(pullback(splat_grads)[0], lax.axis_size("dev"), axis=1)),
+            "dev",
+            0,
+            0,
+        ),
+        axis=1,
     )
     gradient = return_slots(slot_grads, slots_first, local_count)
     new_first = 0.9 * adam_first + 0.1 * gradient

time: 503 us -> 534 us (1.062)
  local copies, waits for them, and re-layouts: 13.9 us -> 31.9 us
  loops' own time: 1.62 us -> 14.4 us
    unnamed x26 -> x56, local copies, waits for them, and re-layouts: 0.34 us -> 19.3 us
    another operation x1, loops' own time: 0.95 us -> 13.8 us  [train_tiles(): lax.scan(train_one_block, jnp.zeros(buffer.shape, buffer.dtype), pieces)]
where the time goes in v1:
time: 534 us; the launch traced here: 525 us
  matrix products  332 us (62%)
  other arithmetic  53.5 us (10%)
  between operations  48.3 us (9%)
  local copies, waits for them, and re-layouts  31.9 us (6%)
  waiting for transfers between devices  28.5 us (5%)
  starting transfers between devices  16.1 us (3%)
  loops' own time  14.4 us (3%)
    dot_general x16, matrix products, pick_one_block(): jnp.dot(source, selector(source.shape[1], block_ids, source.dtype), preci...  121 us
    dot_general x8, matrix products, return_one_block(): lax.dot_general(block_values, choose, (((1,), (1,)), ((), ())), precision...  85.1 us
    dot_general x8, matrix products, block_inputs(): jnp.dot(buffer, choose, precision=lax.Precision.HIGHEST)  41.3 us
    dot_general x4, matrix products, train_one_block(): lax.dot_general(splat_grad, choose, (((1,), (1,)), ((), ())), precision=l...  29.6 us
    dot_general x12, matrix products, composite(): jnp.einsum('bpj,ji->bpi', log_clear, triangle, precision=lax.Precision.HI...  29.2 us
    all_to_all x1, waiting for transfers between devices, shards(): lax.all_to_all(jnp.stack(jnp.split(pullback(splat_grads)[0], lax.axis_siz...  26.1 us
    dot_general x16, matrix products, composite(): jnp.einsum('bpi,cbi->bcp', weight, gathered[6:9], precision=lax.Precision...  24.5 us
    unnamed x56, local copies, waits for them, and re-layouts  19.3 us
  transfers between devices with their start and end apart: 3, of which 3 were waited for; matrix products, arithmetic and copies ran while one was open for 1% of the time, Pallas kernels for 0%

profile of v1, /device:TPU:0, one launch (start us, length us, event | category | flops | bytes accessed | tf_op | source)
XLA Modules:
  0.0 524.5 jit_solution(9010909578788632335)
XLA Ops:
  1.6 60.9 %while.60 = (s32[]{:T(128)}, f32[8,59,512]{2,1,0:T(8,128)S(1)}, s32[8,512]{1,0:T(8,128)S(1)}, f32[59,8192]{1,0:T(8,128)}, s32[]{:T(128)}) while((s32[]{:T(128)}, f32[8,59,512]{2,1,0:T(8,128)S(1)}, s32[8,512]{1,0:T(8,128)S(1)}, f32[59,8192]{1,0:T(8,128)}, s32[]{:T(128)}) %tuple.413), condition=%wide.region_1.2_spmd, body=%wide.region_0.1_spmd.sunk | while | flops 2973761536 | bytes 2070597 | solution.py:321
  1.6 7.6 %fusion.409 = f32[8,59,512]{2,1,0:T(8,128)S(1)} fusion(f32[8,59,512]{2,1,0:T(8,128)S(1)} %get-tuple-element.996, s32[]{:T(128)} %get-tuple-element.995, f32[59,8192]{1,0:T(8,128)} %get-tuple-element.1003, s32[512]{0:T(512)S(1)} %bitcast.1696), kind=kOutput, calls=%fused_computation.6.clone.1 | convolution fusion | flops 2973761536 | bytes 2066436 | tf_op jit(solution)/shard_map/while/body/eval_jaxpr/dot_general | solution.py:315
  9.2 7.6 %fusion.409 = f32[8,59,512]{2,1,0:T(8,128)S(1)} fusion(f32[8,59,512]{2,1,0:T(8,128)S(1)} %get-tuple-element.996, s32[]{:T(128)} %get-tuple-element.995, f32[59,8192]{1,0:T(8,128)} %get-tuple-element.1003, s32[512]{0:T(512)S(1)} %bitcast.1696), kind=kOutput, calls=%fused_computation.6.clone.1 | convolution fusion | flops 2973761536 | bytes 2066436 | tf_op jit(solution)/shard_map/while/body/eval_jaxpr/dot_general | solution.py:315
  16.9 7.6 %fusion.409 = f32[8,59,512]{2,1,0:T(8,128)S(1)} fusion(f32[8,59,512]{2,1,0:T(8,128)S(1)} %get-tuple-element.996, s32[]{:T(128)} %get-tuple-element.995, f32[59,8192]{1,0:T(8,128)} %get-tuple-element.1003, s32[512]{0:T(512)S(1)} %bitcast.1696), kind=kOutput, calls=%fused_computation.6.clone.1 | convolution fusion | flops 2973761536 | bytes 2066436 | tf_op jit(solution)/shard_map/while/body/eval_jaxpr/dot_general | solution.py:315
  24.5 7.6 %fusion.409 = f32[8,59,512]{2,1,0:T(8,128)S(1)} fusion(f32[8,59,512]{2,1,0:T(8,128)S(1)} %get-tuple-element.996, s32[]{:T(128)} %get-tuple-element.995, f32[59,8192]{1,0:T(8,128)} %get-tuple-element.1003, s32[512]{0:T(512)S(1)} %bitcast.1696), kind=kOutput, calls=%fused_computation.6.clone.1 | convolution fusion | flops 2973761536 | bytes 2066436 | tf_op jit(solution)/shard_map/while/body/eval_jaxpr/dot_general | solution.py:315
  32.1 7.6 %fusion.409 = f32[8,59,512]{2,1,0:T(8,128)S(1)} fusion(f32[8,59,512]{2,1,0:T(8,128)S(1)} %get-tuple-element.996, s32[]{:T(128)} %get-tuple-element.995, f32[59,8192]{1,0:T(8,128)} %get-tuple-element.1003, s32[512]{0:T(512)S(1)} %bitcast.1696), kind=kOutput, calls=%fused_computation.6.clone.1 | convolution fusion | flops 2973761536 | bytes 2066436 | tf_op jit(solution)/shard_map/while/body/eval_jaxpr/dot_general | solution.py:315
  39.7 7.6 %fusion.409 = f32[8,59,512]{2,1,0:T(8,128)S(1)} fusion(f32[8,59,512]{2,1,0:T(8,128)S(1)} %get-tuple-element.996, s32[]{:T(128)} %get-tuple-element.995, f32[59,8192]{1,0:T(8,128)} %get-tuple-element.1003, s32[512]{0:T(512)S(1)} %bitcast.1696), kind=kOutput, calls=%fused_computation.6.clone.1 | convolution fusion | flops 2973761536 | bytes 2066436 | tf_op jit(solution)/shard_map/while/body/eval_jaxpr/dot_general | solution.py:315
  47.3 7.6 %fusion.409 = f32[8,59,512]{2,1,0:T(8,128)S(1)} fusion(f32[8,59,512]{2,1,0:T(8,128)S(1)} %get-tuple-element.996, s32[]{:T(128)} %get-tuple-element.995, f32[59,8192]{1,0:T(8,128)} %get-tuple-element.1003, s32[512]{0:T(512)S(1)} %bitcast.1696), kind=kOutput, calls=%fused_computation.6.clone.1 | convolution fusion | flops 2973761536 | bytes 2066436 | tf_op jit(solution)/shard_map/while/body/eval_jaxpr/dot_general | solution.py:315
  54.9 7.6 %fusion.409 = f32[8,59,512]{2,1,0:T(8,128)S(1)} fusion(f32[8,59,512]{2,1,0:T(8,128)S(1)} %get-tuple-element.996, s32[]{:T(128)} %get-tuple-element.995, f32[59,8192]{1,0:T(8,128)} %get-tuple-element.1003, s32[512]{0:T(512)S(1)} %bitcast.1696), kind=kOutput, calls=%fused_computation.6.clone.1 | convolution fusion | flops 2973761536 | bytes 2066436 | tf_op jit(solution)/shard_map/while/body/eval_jaxpr/dot_general | solution.py:315
  64.8 7.3 %all-to-all-start = ((f32[59,32,128]{2,0,1:T(8,128)}), f32[59,32,128]{2,0,1:T(8,128)S(1)}, u32[]{:S(2)}, u32[]{:S(2)}) async-start(f32[59,32,128]{2,0,1:T(8,128)} %copy.48), calls=%async_computation | async-start | bytes 2097152 | tf_op jit(solution)/shard_map/all_to_all | solution.py:379
  98.4 7.6 %broadcast_multiply_fusion.3 = (f32[1,32,128]{2,1,0:T(8,128)S(1)}, f32[1,32,128]{2,1,0:T(8,128)S(1)}, f32[1,32,128]{2,1,0:T(8,128)S(1)}, f32[1,32,128]{2,1,0:T(8...) fusion(f32[]{:T(128)} %bitcast.25, ...), kind=kLoop, calls=%fused_computation.693 | loop fusion | flops 102400 | bytes 196668 | tf_op jit(solution)/shard_map/jvp()/mul | solution.py:156
  110.5 107.2 %while.64 = (s32[]{:T(128)}, f32[9,4096]{1,0:T(8,128)S(1)}, s32[4,8,128]{2,1,0:T(8,128)S(1)}, f32[9,4096]{1,0:T(8,128)S(1)}, s32[4,8]{1,0:T(4,128)S(1)}, /*index...) while((s32[]{:T(128)}, f32[9,4096]{1,0:T(8,128)S(1)}, ...), condition=%wide.region_10.11_spmd.clone.clone, body=%wide.region_3.10_spmd.clone.clone.sunk | while | flops 1775461632 | bytes 7651711 | solution.py:282
  110.9 5.2 fusion.432
  126.8 7.4 %fusion.436 = f32[9,4096]{1,0:T(8,128)S(1)} fusion(f32[9,1024]{1,0:T(8,128)S(1)} %bitcast.1605, s32[1024]{0:T(1024)S(1)} %maximum_bitcast_fusion.5, f32[9,4096]{1,0:T(8,128)S(1)} %get-tuple-element.1015, pred[]{:T(512)S(6)} %compare.134), kind=kOutput, calls=%fused_computation.82.clone.1 | convolution fusion | flops 457252864 | bytes 335873 | tf_op jit(solution)/shard_map/while/body/eval_jaxpr/dot_general | solution.py:271
  134.4 5.2 fusion.432
  150.3 7.4 %fusion.436 = f32[9,4096]{1,0:T(8,128)S(1)} fusion(f32[9,1024]{1,0:T(8,128)S(1)} %bitcast.1605, s32[1024]{0:T(1024)S(1)} %maximum_bitcast_fusion.5, f32[9,4096]{1,0:T(8,128)S(1)} %get-tuple-element.1015, pred[]{:T(512)S(6)} %compare.134), kind=kOutput, calls=%fused_computation.82.clone.1 | convolution fusion | flops 457252864 | bytes 335873 | tf_op jit(solution)/shard_map/while/body/eval_jaxpr/dot_general | solution.py:271
  157.8 5.2 fusion.432
  173.7 7.4 %fusion.436 = f32[9,4096]{1,0:T(8,128)S(1)} fusion(f32[9,1024]{1,0:T(8,128)S(1)} %bitcast.1605, s32[1024]{0:T(1024)S(1)} %maximum_bitcast_fusion.5, f32[9,4096]{1,0:T(8,128)S(1)} %get-tuple-element.1015, pred[]{:T(512)S(6)} %compare.134), kind=kOutput, calls=%fused_computation.82.clone.1 | convolution fusion | flops 457252864 | bytes 335873 | tf_op jit(solution)/shard_map/while/body/eval_jaxpr/dot_general | solution.py:271
  181.3 5.2 fusion.432
  197.2 7.4 %fusion.436 = f32[9,4096]{1,0:T(8,128)S(1)} fusion(f32[9,1024]{1,0:T(8,128)S(1)} %bitcast.1605, s32[1024]{0:T(1024)S(1)} %maximum_bitcast_fusion.5, f32[9,4096]{1,0:T(8,128)S(1)} %get-tuple-element.1015, pred[]{:T(512)S(6)} %compare.134), kind=kOutput, calls=%fused_computation.82.clone.1 | convolution fusion | flops 457252864 | bytes 335873 | tf_op jit(solution)/shard_map/while/body/eval_jaxpr/dot_general | solution.py:271
  219.5 6.4 %broadcast_multiply_fusion.28 = (f32[1,4096]{1,0:T(1,128)S(1)}, f32[1,4096]{1,0:T(1,128)S(1)}, f32[1,4096]{1,0:T(1,128)S(1)}, f32[1,4096]{1,0:T(1,128)S(1)}, f32...) fusion(f32[]{:T(128)} %bitcast.35, f32[1,4096]{1,0:T(1,128)S(1)} %bitcast.1681, ...), kind=kLoop, calls=%fused_computation.725 | loop fusion | flops 585728 | bytes 884772 | tf_op jit(solution)/shard_map/transpose(jvp())/mul | solution.py:107
  257.8 5.0 all-to-all-start.1
  262.9 26.1 %all-to-all-done.1 = f32[32,59,128]{2,1,0:T(8,128)S(1)} async-done(((f32[32,59,128]{2,1,0:T(8,128)}), f32[32,59,128]{2,1,0:T(8,128)S(1)}, u32[]{:S(2)}, u32[]{:S(2)}) %all-to-all-start.1) | async-done | bytes 966688 | tf_op jit(solution)/shard_map/all_to_all | solution.py:383
  289.9 86.1 %while.63 = (s32[]{:T(128)}, f32[59,8192]{1,0:T(8,128)}, f32[8,59,512]{2,0,1:T(8,128)S(1)}, s32[8,512]{1,0:T(8,128)S(1)}, s32[]{:T(128)}, /*index=5*/s32[]{:T(128)}) while((s32[]{:T(128)}, f32[59,8192]{1,0:T(8,128)}, f32[8,59,512]{2,0,1:T(8,128)S(1)}, s32[8,512]{1,0:T(8,128)S(1)}, s32[]{:T(128)}, /*index=5*/s32[]{:T(128)}) %tuple.431), condition=%wide.region_13.14_spmd.clone, body=%wide.region_12.13_spmd.clone.sunk | while | flops 2974728192 | bytes 4235351 | solution.py:345
  290.0 9.6 %fusion.421 = f32[59,8192]{1,0:T(8,128)} fusion(s32[512]{0:T(512)S(1)} %bitcast.1695, f32[59,8192]{1,0:T(8,128)} %get-tuple-element.1039, pred[]{:T(512)S(6)} %compare.133, f32[1,59,512]{2,0,1:T(1,128)S(1)} %constant_dynamic-slice_fusion.13), kind=kOutput, calls=%fused_computation.72.clone.1 | convolution fusion | flops 2974728192 | bytes 3989505 | tf_op jit(solution)/shard_map/while/body/eval_jaxpr/dot_general | solution.py:339
  299.7 10.8 %fusion.421 = f32[59,8192]{1,0:T(8,128)} fusion(s32[512]{0:T(512)S(1)} %bitcast.1695, f32[59,8192]{1,0:T(8,128)} %get-tuple-element.1039, pred[]{:T(512)S(6)} %compare.133, f32[1,59,512]{2,0,1:T(1,128)S(1)} %constant_dynamic-slice_fusion.13), kind=kOutput, calls=%fused_computation.72.clone.1 | convolution fusion | flops 2974728192 | bytes 3989505 | tf_op jit(solution)/shard_map/while/body/eval_jaxpr/dot_general | solution.py:339
  310.6 10.8 %fusion.421 = f32[59,8192]{1,0:T(8,128)} fusion(s32[512]{0:T(512)S(1)} %bitcast.1695, f32[59,8192]{1,0:T(8,128)} %get-tuple-element.1039, pred[]{:T(512)S(6)} %compare.133, f32[1,59,512]{2,0,1:T(1,128)S(1)} %constant_dynamic-slice_fusion.13), kind=kOutput, calls=%fused_computation.72.clone.1 | convolution fusion | flops 2974728192 | bytes 3989505 | tf_op jit(solution)/shard_map/while/body/eval_jaxpr/dot_general | solution.py:339
  321.5 10.8 %fusion.421 = f32[59,8192]{1,0:T(8,128)} fusion(s32[512]{0:T(512)S(1)} %bitcast.1695, f32[59,8192]{1,0:T(8,128)} %get-tuple-element.1039, pred[]{:T(512)S(6)} %compare.133, f32[1,59,512]{2,0,1:T(1,128)S(1)} %constant_dynamic-slice_fusion.13), kind=kOutput, calls=%fused_computation.72.clone.1 | convolution fusion | flops 2974728192 | bytes 3989505 | tf_op jit(solution)/shard_map/while/body/eval_jaxpr/dot_general | solution.py:339
  332.5 10.8 %fusion.421 = f32[59,8192]{1,0:T(8,128)} fusion(s32[512]{0:T(512)S(1)} %bitcast.1695, f32[59,8192]{1,0:T(8,128)} %get-tuple-element.1039, pred[]{:T(512)S(6)} %compare.133, f32[1,59,512]{2,0,1:T(1,128)S(1)} %constant_dynamic-slice_fusion.13), kind=kOutput, calls=%fused_computation.72.clone.1 | convolution fusion | flops 2974728192 | bytes 3989505 | tf_op jit(solution)/shard_map/while/body/eval_jaxpr/dot_general | solution.py:339
  343.4 10.8 %fusion.421 = f32[59,8192]{1,0:T(8,128)} fusion(s32[512]{0:T(512)S(1)} %bitcast.1695, f32[59,8192]{1,0:T(8,128)} %get-tuple-element.1039, pred[]{:T(512)S(6)} %compare.133, f32[1,59,512]{2,0,1:T(1,128)S(1)} %constant_dynamic-slice_fusion.13), kind=kOutput, calls=%fused_computation.72.clone.1 | convolution fusion | flops 2974728192 | bytes 3989505 | tf_op jit(solution)/shard_map/while/body/eval_jaxpr/dot_general | solution.py:339
  354.3 10.8 %fusion.421 = f32[59,8192]{1,0:T(8,128)} fusion(s32[512]{0:T(512)S(1)} %bitcast.1695, f32[59,8192]{1,0:T(8,128)} %get-tuple-element.1039, pred[]{:T(512)S(6)} %compare.133, f32[1,59,512]{2,0,1:T(1,128)S(1)} %constant_dynamic-slice_fusion.13), kind=kOutput, calls=%fused_computation.72.clone.1 | convolution fusion | flops 2974728192 | bytes 3989505 | tf_op jit(solution)/shard_map/while/body/eval_jaxpr/dot_general | solution.py:339
  365.2 10.8 %fusion.421 = f32[59,8192]{1,0:T(8,128)} fusion(s32[512]{0:T(512)S(1)} %bitcast.1695, f32[59,8192]{1,0:T(8,128)} %get-tuple-element.1039, pred[]{:T(512)S(6)} %compare.133, f32[1,59,512]{2,0,1:T(1,128)S(1)} %constant_dynamic-slice_fusion.13), kind=kOutput, calls=%fused_computation.72.clone.1 | convolution fusion | flops 2974728192 | bytes 3989505 | tf_op jit(solution)/shard_map/while/body/eval_jaxpr/dot_general | solution.py:339
  376.0 6.3 %divide_subtract_fusion = (f32[59,8192]{1,0:T(8,128)}, f32[59,8192]{1,0:T(8,128)}, f32[59,8192]{1,0:T(8,128)}) fusion(f32[59,8192]{1,0:T(8,128)S(1)} %copy-done, f32[59]{0:T(128)S(1)} %copy-done.7, f32[59,8192]{1,0:T(8,128)} %get-tuple-element.318, f32[59,8192]{1,0:T(8,128)} %param.23, f32[59,8192]{1,0:T(8,128)} %param.24), kind=kLoop, calls=%fused_computation.164 | loop fusion | flops 5799936 | bytes 13533420 | tf_op jit(solution)/shard_map/sub | solution.py:395
  382.5 60.9 %while.61 = (s32[]{:T(128)}, f32[8,59,512]{2,1,0:T(8,128)S(1)}, s32[8,512]{1,0:T(8,128)S(1)}, f32[59,8192]{1,0:T(8,128)}, s32[]{:T(128)}) while((s32[]{:T(128)}, f32[8,59,512]{2,1,0:T(8,128)S(1)}, s32[8,512]{1,0:T(8,128)S(1)}, f32[59,8192]{1,0:T(8,128)}, s32[]{:T(128)}) %tuple.422), condition=%wide.region_15.16_spmd, body=%wide.region_14.15_spmd.sunk | while | flops 2973761536 | bytes 2070597 | solution.py:321
  382.5 7.6 %fusion.411 = f32[8,59,512]{2,1,0:T(8,128)S(1)} fusion(f32[8,59,512]{2,1,0:T(8,128)S(1)} %get-tuple-element.1056, s32[]{:T(128)} %get-tuple-element.1055, f32[59,8192]{1,0:T(8,128)} %get-tuple-element.1063, s32[512]{0:T(512)S(1)} %bitcast.1697), kind=kOutput, calls=%fused_computation.12.clone.1 | convolution fusion | flops 2973761536 | bytes 2066436 | tf_op jit(solution)/shard_map/while/body/eval_jaxpr/dot_general | solution.py:315
  390.1 7.6 %fusion.411 = f32[8,59,512]{2,1,0:T(8,128)S(1)} fusion(f32[8,59,512]{2,1,0:T(8,128)S(1)} %get-tuple-element.1056, s32[]{:T(128)} %get-tuple-element.1055, f32[59,8192]{1,0:T(8,128)} %get-tuple-element.1063, s32[512]{0:T(512)S(1)} %bitcast.1697), kind=kOutput, calls=%fused_computation.12.clone.1 | convolution fusion | flops 2973761536 | bytes 2066436 | tf_op jit(solution)/shard_map/while/body/eval_jaxpr/dot_general | solution.py:315
  397.7 7.6 %fusion.411 = f32[8,59,512]{2,1,0:T(8,128)S(1)} fusion(f32[8,59,512]{2,1,0:T(8,128)S(1)} %get-tuple-element.1056, s32[]{:T(128)} %get-tuple-element.1055, f32[59,8192]{1,0:T(8,128)} %get-tuple-element.1063, s32[512]{0:T(512)S(1)} %bitcast.1697), kind=kOutput, calls=%fused_computation.12.clone.1 | convolution fusion | flops 2973761536 | bytes 2066436 | tf_op jit(solution)/shard_map/while/body/eval_jaxpr/dot_general | solution.py:315
  405.3 7.6 %fusion.411 = f32[8,59,512]{2,1,0:T(8,128)S(1)} fusion(f32[8,59,512]{2,1,0:T(8,128)S(1)} %get-tuple-element.1056, s32[]{:T(128)} %get-tuple-element.1055, f32[59,8192]{1,0:T(8,128)} %get-tuple-element.1063, s32[512]{0:T(512)S(1)} %bitcast.1697), kind=kOutput, calls=%fused_computation.12.clone.1 | convolution fusion | flops 2973761536 | bytes 2066436 | tf_op jit(solution)/shard_map/while/body/eval_jaxpr/dot_general | solution.py:315
  412.9 7.6 %fusion.411 = f32[8,59,512]{2,1,0:T(8,128)S(1)} fusion(f32[8,59,512]{2,1,0:T(8,128)S(1)} %get-tuple-element.1056, s32[]{:T(128)} %get-tuple-element.1055, f32[59,8192]{1,0:T(8,128)} %get-tuple-element.1063, s32[512]{0:T(512)S(1)} %bitcast.1697), kind=kOutput, calls=%fused_computation.12.clone.1 | convolution fusion | flops 2973761536 | bytes 2066436 | tf_op jit(solution)/shard_map/while/body/eval_jaxpr/dot_general | solution.py:315
  420.5 7.6 %fusion.411 = f32[8,59,512]{2,1,0:T(8,128)S(1)} fusion(f32[8,59,512]{2,1,0:T(8,128)S(1)} %get-tuple-element.1056, s32[]{:T(128)} %get-tuple-element.1055, f32[59,8192]{1,0:T(8,128)} %get-tuple-element.1063, s32[512]{0:T(512)S(1)} %bitcast.1697), kind=kOutput, calls=%fused_computation.12.clone.1 | convolution fusion | flops 2973761536 | bytes 2066436 | tf_op jit(solution)/shard_map/while/body/eval_jaxpr/dot_general | solution.py:315
  428.2 7.6 %fusion.411 = f32[8,59,512]{2,1,0:T(8,128)S(1)} fusion(f32[8,59,512]{2,1,0:T(8,128)S(1)} %get-tuple-element.1056, s32[]{:T(128)} %get-tuple-element.1055, f32[59,8192]{1,0:T(8,128)} %get-tuple-element.1063, s32[512]{0:T(512)S(1)} %bitcast.1697), kind=kOutput, calls=%fused_computation.12.clone.1 | convolution fusion | flops 2973761536 | bytes 2066436 | tf_op jit(solution)/shard_map/while/body/eval_jaxpr/dot_general | solution.py:315
  435.8 7.6 %fusion.411 = f32[8,59,512]{2,1,0:T(8,128)S(1)} fusion(f32[8,59,512]{2,1,0:T(8,128)S(1)} %get-tuple-element.1056, s32[]{:T(128)} %get-tuple-element.1055, f32[59,8192]{1,0:T(8,128)} %get-tuple-element.1063, s32[512]{0:T(512)S(1)} %bitcast.1697), kind=kOutput, calls=%fused_computation.12.clone.1 | convolution fusion | flops 2973761536 | bytes 2066436 | tf_op jit(solution)/shard_map/while/body/eval_jaxpr/dot_general | solution.py:315
  475.7 7.6 %broadcast_multiply_fusion.1 = (f32[1,32,128]{2,1,0:T(8,128)S(1)}, f32[1,32,128]{2,1,0:T(8,128)S(1)}, f32[1,32,128]{2,1,0:T(8,128)S(1)}, f32[1,32,128]{2,1,0:T(8...) fusion(f32[]{:T(128)} %bitcast.165, ...), kind=kLoop, calls=%fused_computation.691 | loop fusion | flops 98304 | bytes 180284 | tf_op jit(solution)/shard_map/mul | solution.py:156
  488.2 36.0 %while.62 = (s32[]{:T(128)}, f32[4,8,3,256]{3,1,0,2:T(8,128)}, s32[4,8,128]{2,1,0:T(8,128)S(1)}, f32[9,4096]{1,0:T(8,128)S(1)}, s32[4,8]{1,0:T(4,128)S(1)}, /*index=5*/s32[]{:T(128)}) while((s32[]{:T(128)}, f32[4,8,3,256]{3,1,0,2:T(8,128)}, s32[4,8,128]{2,1,0:T(8,128)S(1)}, f32[9,4096]{1,0:T(8,128)S(1)}, s32[4,8]{1,0:T(4,128)S(1)}, ...), condition=%wide.region_18.19_spmd.clone, body=%wide.region_17.18_spmd.clone.sunk | while | flops 876660928 | bytes 2507605 | solution.py:295
  488.3 5.2 fusion.416
  497.3 5.2 fusion.416
  506.3 5.2 fusion.416
  515.3 5.2 fusion.416
  (300 shorter events, 118.1 us)
Async XLA Ops:
  63.2 8.9 %copy-start.5 = (f32[2,6]{1,0:T(2,128)S(1)}, f32[2,6]{1,0:T(2,128)}, u32[]{:S(2)}) copy-start(f32[2,6]{1,0:T(2,128)} %param.25) | copy-start | bytes 148
  63.2 14.1 %copy-start.10 = (f32[1,3]{1,0:T(1,128)S(1)}, f32[1,3]{1,0:T(1,128)}, u32[]{:S(2)}) copy-start(f32[1,3]{1,0:T(1,128)} %constant.324.clone.1) | copy-start | bytes 40
  63.2 14.1 %copy-start.11 = (f32[1,3]{1,0:T(1,128)S(1)}, f32[1,3]{1,0:T(1,128)}, u32[]{:S(2)}) copy-start(f32[1,3]{1,0:T(1,128)} %constant.325.clone.1) | copy-start | bytes 40
  63.2 14.2 %copy-start.6 = (f32[1,3]{1,0:T(1,128)S(1)}, f32[1,3]{1,0:T(1,128)}, u32[]{:S(2)}) copy-start(f32[1,3]{1,0:T(1,128)} %constant.323.clone.1) | copy-start | bytes 40
  63.2 34.1 %copy-start.3 = (f32[32,3,256]{2,0,1:T(8,128)S(1)}, f32[32,3,256]{2,0,1:T(8,128)}, u32[]{:S(2)}) copy-start(f32[32,3,256]{2,0,1:T(8,128)} %param.32) | copy-start | bytes 294916
  63.2 34.1 %copy-start.8 = (s32[32]{0:T(128)S(1)}, s32[32]{0:T(128)}, u32[]{:S(2)}) copy-start(s32[32]{0:T(128)} %param.30) | copy-start | bytes 388
  64.8 33.5 %all-to-all-start = ((f32[59,32,128]{2,0,1:T(8,128)}), f32[59,32,128]{2,0,1:T(8,128)S(1)}, u32[]{:S(2)}, u32[]{:S(2)}) async-start(f32[59,32,128]{2,0,1:T(8,128)} %copy.48), calls=%async_computation | async-start | bytes 2097152 | tf_op jit(solution)/shard_map/all_to_all | solution.py:379
  92.2 18.3 %copy-start.1 = (s32[32,128]{1,0:T(8,128)S(1)}, s32[32,128]{1,0:T(8,128)}, u32[]{:S(2)}) copy-start(s32[32,128]{1,0:T(8,128)} %param.28) | copy-start | bytes 49156
  238.0 24.8 %copy-start.4 = (s32[1,4096]{1,0:T(1,128)S(1)}, s32[1,4096]{1,0:T(1,128)}, u32[]{:S(2)}) copy-start(s32[1,4096]{1,0:T(1,128)} %param.26) | copy-start | bytes 49156
  257.8 31.2 %all-to-all-start.1 = ((f32[32,59,128]{2,1,0:T(8,128)}), f32[32,59,128]{2,1,0:T(8,128)S(1)}, u32[]{:S(2)}, u32[]{:S(2)}) async-start(f32[32,59,128]{2,1,0:T(8,128)} %constant_dynamic-update-slice_fusion), calls=%async_computation.1 | async-start | bytes 2097152 | tf_op jit(solution)/shard_map/all_to_all | solution.py:383
  289.8 86.2 %copy-start = (f32[59,8192]{1,0:T(8,128)S(1)}, f32[59,8192]{1,0:T(8,128)}, u32[]{:S(2)}) copy-start(f32[59,8192]{1,0:T(8,128)} %get-tuple-element.1086) | copy-start | bytes 5799940
  289.8 86.2 %copy-start.7 = (f32[59]{0:T(128)S(1)}, f32[59]{0:T(128)}, u32[]{:S(2)}) copy-start(f32[59]{0:T(128)} %constant.528) | copy-start | bytes 712
  444.0 29.9 %copy-start.9 = (s32[32]{0:T(128)S(1)}, s32[32]{0:T(128)}, u32[]{:S(2)}) copy-start(s32[32]{0:T(128)} %param.31) | copy-start | bytes 388
  445.6 30.0 %all-to-all-start.2 = ((f32[59,32,128]{2,0,1:T(8,128)}), f32[59,32,128]{2,0,1:T(8,128)S(1)}, u32[]{:S(2)}, u32[]{:S(2)}) async-start(f32[59,32,128]{2,0,1:T(8,128)} %copy.57), calls=%async_computation.2 | async-start | bytes 2097152 | tf_op jit(solution)/shard_map/all_to_all | solution.py:400
  449.4 38.7 %copy-start.2 = (s32[32,128]{1,0:T(8,128)S(1)}, s32[32,128]{1,0:T(8,128)}, u32[]{:S(2)}) copy-start(s32[32,128]{1,0:T(8,128)} %param.29) | copy-start | bytes 49156
